TPU v7x, 32 devices: a whole 2x2x4 slice. The times are simulated.
32 devices in a mesh: dp: 8 (over z, y), sy: 2 (over x), sx: 2 (over core).
Axes of the slice: x: 2, y: 2, z: 4, core: 2. Of those that a mesh axis runs over, the one named last changes fastest.
Arguments:
- features: bfloat16 [8, 56, 56, 256], P('dp', 'sy', 'sx'), may hold values from -8 to 8
- labels: int32 [8], P('dp'), may hold values from 0 to 999
- grid: int32 [2], replicated, may hold values from 0 to 49
- w_reduce: bfloat16 [3, 256, 64], P(None, None, 'dp'), may hold values from -0.375 to 0.375
- w_spatial: bfloat16 [3, 3, 3, 64, 64], P(None, None, None, None, 'dp'), may hold values from -0.25 to 0.25
- w_expand: bfloat16 [3, 64, 256], P(None, None, 'dp'), may hold values from -0.75 to 0.75
- w_class: bfloat16 [256, 1000], P('dp'), may hold values from -1.5 to 1.5
- dir_reduce: bfloat16 [2, 3, 256, 64], P(None, None, None, 'dp'), may hold values from -6 to 6
- dir_spatial: bfloat16 [2, 3, 3, 3, 64, 64], P(None, None, None, None, None, 'dp'), may hold values from -6 to 6
- dir_expand: bfloat16 [2, 3, 64, 256], P(None, None, None, 'dp'), may hold values from -6 to 6
- dir_class: bfloat16 [2, 256, 1000], P(None, 'dp'), may hold values from -6 to 6
- gain_mid: float32 [3, 2, 64], replicated, may hold values from 0.5 to 1.5
- shift_mid: float32 [3, 2, 64], replicated, may hold values from -3 to 3
- gain_out: float32 [3, 256], replicated, may hold values from 0.5 to 1.5
- shift_out: float32 [3, 256], replicated, may hold values from -3 to 3
Outputs:
- section_out: bfloat16 [8, 56, 56, 256], P('dp', 'sy', 'sx')
- image_loss: float32 [8], P('dp')
- mean_loss: float32 [], replicated
All inputs are finite; a program needn't handle non-finite values.
Results may differ from a plain program's by a relative error of at most 0.012.
Values may be sent and summed in bfloat16 or wider, within the bound.
A program may use at most 64 MiB of HBM per device.

v0:
```python
import jax
import jax.numpy as jnp
from jax import lax
from jax.sharding import PartitionSpec as P

BLOCKS = 3
GRID = 50
EPS_NORM = 1e-06
EPS_BN = 1e-05


def extended(cells, sides, width):
    for axis, dim in sides:
        count = lax.axis_size(axis)
        ends = count - 1
        head = lax.slice_in_dim(cells, 0, width, axis=dim)
        tail = lax.slice_in_dim(cells, cells.shape[dim] - width, cells.shape[dim], axis=dim)
        cells = jnp.concatenate(
            [
                lax.ppermute(tail, axis, [(i, (i + 1) % count) for i in range(ends)]),
                cells,
                lax.ppermute(head, axis, [((i + 1) % count, i) for i in range(ends)]),
            ],
            axis=dim,
        )
    return cells


def coefficients(grid):
    values = grid.astype(jnp.float32)
    alpha = (2.0 * values + 1.0 - GRID) / GRID
    return (alpha[0], alpha[1])


def filter_ratio(base, direction):
    base_norm = jnp.sqrt(jnp.sum(jnp.square(base.astype(jnp.float32)), axis=0, keepdims=True))
    dir_norm = jnp.sqrt(
        jnp.sum(jnp.square(direction.astype(jnp.float32)), axis=0, keepdims=True) + EPS_NORM
    )
    return base_norm / dir_norm


def combine_filters(base, dir_a, dir_b, alpha_a, alpha_b):
    ratio_a = filter_ratio(base, dir_a)
    ratio_b = filter_ratio(base, dir_b)
    value = (
        base.astype(jnp.float32)
        + alpha_a * ratio_a * dir_a.astype(jnp.float32)
        + alpha_b * ratio_b * dir_b.astype(jnp.float32)
    )
    return value.astype(jnp.bfloat16)


def perturbed_product(left, base, dir_a, dir_b, alpha_a, alpha_b):
    local = combine_filters(base, dir_a, dir_b, alpha_a, alpha_b)
    return jnp.dot(
        left, lax.all_gather(local, "dp", axis=1, tiled=True), preferred_element_type=jnp.float32
    )


def normalize(y, gain, shift, count):
    mean = lax.psum(jnp.sum(y, axis=0), ("dp", "sy", "sx")) / count
    centred = y - mean
    var = lax.psum(jnp.sum(centred * centred, axis=0), ("dp", "sy", "sx")) / count
    return centred * lax.rsqrt(var + EPS_BN) * gain + shift


def padded_tile(inner):
    return extended(inner, (("sy", 1), ("sx", 2)), 1)


def per_device(
    features,
    labels,
    grid,
    w_reduce,
    w_spatial,
    w_expand,
    w_class,
    dir_reduce,
    dir_spatial,
    dir_expand,
    dir_class,
    gain_mid,
    shift_mid,
    gain_out,
    shift_out,
):
    alpha_a, alpha_b = coefficients(grid)
    images, rows, cols, width = features.shape
    tiles = lax.axis_size("sy") * lax.axis_size("sx")
    count = images * rows * cols * lax.axis_size("dp") * tiles
    inner_width = w_spatial.shape[3]
    current = features
    for block in range(BLOCKS):
        flat = current.reshape(-1, width)
        first = perturbed_product(
            flat, w_reduce[block], dir_reduce[0, block], dir_reduce[1, block], alpha_a, alpha_b
        )
        first = jax.nn.relu(
            normalize(first, gain_mid[block, 0], shift_mid[block, 0], count)
        ).astype(jnp.bfloat16)
        framed = padded_tile(first.reshape(images, rows, cols, inner_width))
        patches = jnp.concatenate(
            [framed[:, i : i + rows, j : j + cols, :] for i in range(3) for j in range(3)], axis=-1
        )
        patches = patches.reshape(-1, 9 * inner_width)
        spatial_base = w_spatial[block].reshape(9 * inner_width, -1)
        spatial_a = dir_spatial[0, block].reshape(9 * inner_width, -1)
        spatial_b = dir_spatial[1, block].reshape(9 * inner_width, -1)
        second = perturbed_product(patches, spatial_base, spatial_a, spatial_b, alpha_a, alpha_b)
        second = jax.nn.relu(
            normalize(second, gain_mid[block, 1], shift_mid[block, 1], count)
        ).astype(jnp.bfloat16)
        third = perturbed_product(
            second, w_expand[block], dir_expand[0, block], dir_expand[1, block], alpha_a, alpha_b
        )
        third = normalize(third, gain_out[block], shift_out[block], count)
        current = (
            jax.nn.relu(flat.astype(jnp.float32) + third)
            .astype(jnp.bfloat16)
            .reshape(images, rows, cols, width)
        )
    pooled_part = jnp.sum(current.astype(jnp.float32), axis=(1, 2))
    pooled = (lax.psum(pooled_part, ("sy", "sx")) / (rows * cols * tiles)).astype(jnp.bfloat16)
    class_a = dir_class[0]
    class_b = dir_class[1]
    norm_base, norm_a, norm_b = lax.psum(
        (
            jnp.sum(jnp.square(w_class.astype(jnp.float32)), axis=0),
            jnp.sum(jnp.square(class_a.astype(jnp.float32)), axis=0),
            jnp.sum(jnp.square(class_b.astype(jnp.float32)), axis=0),
        ),
        "dp",
    )
    ratio_a = jnp.sqrt(norm_base) / jnp.sqrt(norm_a + EPS_NORM)
    ratio_b = jnp.sqrt(norm_base) / jnp.sqrt(norm_b + EPS_NORM)
    local_class = (
        w_class.astype(jnp.float32)
        + alpha_a * ratio_a * class_a.astype(jnp.float32)
        + alpha_b * ratio_b * class_b.astype(jnp.float32)
    ).astype(jnp.bfloat16)
    logits = jnp.dot(
        pooled,
        lax.all_gather(local_class, "dp", axis=0, tiled=True),
        preferred_element_type=jnp.float32,
    )
    summed = jnp.log(jnp.sum(jnp.exp(logits), axis=1))
    classes = lax.broadcasted_iota(jnp.int32, logits.shape, 1)
    picked = jnp.sum(jnp.where(classes == labels[:, None], logits, 0.0), axis=1)
    image_loss = summed - picked
    mean_loss = lax.psum(jnp.sum(image_loss), "dp") / (images * lax.axis_size("dp"))
    return (current, image_loss, mean_loss)


def solution(mesh):
    in_specs = (
        P("dp", "sy", "sx", None),
        P("dp"),
        P(),
        P(None, None, "dp"),
        P(None, None, None, None, "dp"),
        P(None, None, "dp"),
        P("dp", None),
        P(None, None, None, "dp"),
        P(None, None, None, None, None, "dp"),
        P(None, None, None, "dp"),
        P(None, "dp", None),
        P(),
        P(),
        P(),
        P(),
    )
    out_specs = (P("dp", "sy", "sx", None), P("dp"), P())
    return jax.shard_map(
        per_device, mesh=mesh, in_specs=in_specs, out_specs=out_specs, check_vma=False
    )
```

profile of v0, /device:TPU:0, one launch (start us, length us, event | category | flops | bytes accessed | tf_op | source)
XLA Modules:
  0.0 1203.1 jit_solution(10325314932056759414)
XLA Ops:
  4.7 1.3 multiply_multiply_fusion.5
  6.1 1.3 multiply_multiply_fusion.11
  7.4 1.3 multiply_multiply_fusion.17
  8.8 32.4 %all_gather.30 = bf16[256,64]{0,1:T(8,128)(2,1)S(1)} all-gather(bf16[256,8]{0,1:T(8,128)(2,1)S(1)} %get-tuple-element.100), channel_id=1, replica_groups=mesh['dp'=8,'sy'=2,'sx'=2] {'dp'}, dimensions={1}, use_global_device_ids=true | all-gather | bytes 36864 | tf_op jit(solution)/shard_map/all_gather | solution.py:57
  42.7 39.6 %psum.161 = f32[64]{0:T(128)S(1)} all-reduce(f32[64]{0:T(128)S(1)} %get-tuple-element.142), channel_id=1, replica_groups=mesh['dp'=8,'sy'=2,'sx'=2] {'dp','sy','sx'}, use_global_device_ids=true, to_apply=%region_4.0 | all-reduce | flops 64 | bytes 512 | tf_op jit(solution)/shard_map/psum | solution.py:62
  82.4 40.7 %psum.162 = f32[64]{0:T(128)S(1)} all-reduce(f32[64]{0:T(128)S(1)} %multiply_reduce_fusion.8), channel_id=1, replica_groups=mesh['dp'=8,'sy'=2,'sx'=2] {'dp','sy','sx'}, use_global_device_ids=true, to_apply=%region_6.0 | all-reduce | flops 64 | bytes 512 | tf_op jit(solution)/shard_map/psum | solution.py:64
  124.7 4.2 collective-permute-start
  128.8 1.3 collective-permute-start.1
  130.6 32.7 %all_gather.31 = bf16[576,64]{0,1:T(8,128)(2,1)} all-gather(bf16[576,8]{0,1:T(8,128)(2,1)S(1)} %add_convert_fusion.2), channel_id=1, replica_groups=mesh['dp'=8,'sy'=2,'sx'=2] {'dp'}, dimensions={1}, use_global_device_ids=true | all-gather | bytes 82944 | tf_op jit(solution)/shard_map/all_gather | solution.py:57
  166.4 32.6 %all_gather.34 = bf16[576,64]{0,1:T(8,128)(2,1)} all-gather(bf16[576,8]{0,1:T(8,128)(2,1)S(1)} %add_convert_fusion.1), channel_id=1, replica_groups=mesh['dp'=8,'sy'=2,'sx'=2] {'dp'}, dimensions={1}, use_global_device_ids=true | all-gather | bytes 82944 | tf_op jit(solution)/shard_map/all_gather | solution.py:57
  200.1 36.1 %all-reduce = (f32[1000]{0:T(1024)S(1)}, f32[1000]{0:T(1024)S(1)}, f32[1000]{0:T(1024)S(1)}) all-reduce(f32[1000]{0:T(1024)S(1)} %get-tuple-element.4, f32[1000]{0:T(1024)S(1)} %get-tuple-element.174, f32[1000]{0:T(1024)S(1)} %get-tuple-element.3), channel_id=1, replica_groups=mesh['dp'=8,'sy'=2,'sx'=2] {'dp'}, use_global_device_ids=true, to_apply=%region_70.71 | all-reduce | flops 3000 | bytes 24000 | tf_op jit(solution)/shard_map/psum | solution.py:128
  236.2 1.3 multiply_multiply_fusion.1
  237.6 31.2 %all_gather.39 = bf16[256,1000]{1,0:T(8,128)(2,1)S(1)} all-gather(bf16[32,1000]{1,0:T(8,128)(2,1)S(1)} %fusion.14), channel_id=1, replica_groups=mesh['dp'=8,'sy'=2,'sx'=2] {'dp'}, dimensions={0}, use_global_device_ids=true | all-gather | bytes 576000 | tf_op jit(solution)/shard_map/all_gather | solution.py:145
  268.8 1.3 multiply_multiply_fusion.15
  270.2 1.3 multiply_multiply_fusion.3
  272.2 32.5 %all_gather.32 = bf16[64,256]{0,1:T(8,128)(2,1)} all-gather(bf16[64,32]{0,1:T(8,128)(2,1)S(1)} %get-tuple-element.95), channel_id=1, replica_groups=mesh['dp'=8,'sy'=2,'sx'=2] {'dp'}, dimensions={1}, use_global_device_ids=true | all-gather | bytes 36864 | tf_op jit(solution)/shard_map/all_gather | solution.py:57
  306.2 1.3 collective-permute-start.3
  307.5 32.1 %all_gather.33 = bf16[256,64]{0,1:T(8,128)(2,1)} all-gather(bf16[256,8]{0,1:T(8,128)(2,1)S(1)} %get-tuple-element.101), channel_id=1, replica_groups=mesh['dp'=8,'sy'=2,'sx'=2] {'dp'}, dimensions={1}, use_global_device_ids=true | all-gather | bytes 36864 | tf_op jit(solution)/shard_map/all_gather | solution.py:57
  348.3 37.4 %psum.163 = f32[64]{0:T(128)S(1)} all-reduce(f32[64]{0:T(128)S(1)} %get-tuple-element.144), channel_id=1, replica_groups=mesh['dp'=8,'sy'=2,'sx'=2] {'dp','sy','sx'}, use_global_device_ids=true, to_apply=%region_11.12 | all-reduce | flops 64 | bytes 512 | tf_op jit(solution)/shard_map/psum | solution.py:62
  386.0 42.8 %psum.164 = f32[64]{0:T(128)S(1)} all-reduce(f32[64]{0:T(128)S(1)} %multiply_reduce_fusion.7), channel_id=1, replica_groups=mesh['dp'=8,'sy'=2,'sx'=2] {'dp','sy','sx'}, use_global_device_ids=true, to_apply=%region_13.14 | all-reduce | flops 64 | bytes 512 | tf_op jit(solution)/shard_map/psum | solution.py:64
  429.9 38.1 %psum.165 = f32[256]{0:T(256)S(1)} all-reduce(f32[256]{0:T(256)S(1)} %get-tuple-element.146), channel_id=1, replica_groups=mesh['dp'=8,'sy'=2,'sx'=2] {'dp','sy','sx'}, use_global_device_ids=true, to_apply=%region_18.19 | all-reduce | flops 256 | bytes 2048 | tf_op jit(solution)/shard_map/psum | solution.py:62
  468.1 41.9 %psum.166 = f32[256]{0:T(256)S(1)} all-reduce(f32[256]{0:T(256)S(1)} %multiply_reduce_fusion.2), channel_id=1, replica_groups=mesh['dp'=8,'sy'=2,'sx'=2] {'dp','sy','sx'}, use_global_device_ids=true, to_apply=%region_20.21 | all-reduce | flops 256 | bytes 2048 | tf_op jit(solution)/shard_map/psum | solution.py:64
  511.8 38.3 %psum.167 = f32[64]{0:T(128)S(1)} all-reduce(f32[64]{0:T(128)S(1)} %get-tuple-element.148), channel_id=1, replica_groups=mesh['dp'=8,'sy'=2,'sx'=2] {'dp','sy','sx'}, use_global_device_ids=true, to_apply=%region_25.26 | all-reduce | flops 64 | bytes 512 | tf_op jit(solution)/shard_map/psum | solution.py:62
  550.2 41.9 %psum.168 = f32[64]{0:T(128)S(1)} all-reduce(f32[64]{0:T(128)S(1)} %multiply_reduce_fusion.6), channel_id=1, replica_groups=mesh['dp'=8,'sy'=2,'sx'=2] {'dp','sy','sx'}, use_global_device_ids=true, to_apply=%region_27.28 | all-reduce | flops 64 | bytes 512 | tf_op jit(solution)/shard_map/psum | solution.py:64
  593.1 4.2 collective-permute-start.4
  597.3 32.5 %all_gather.35 = bf16[64,256]{0,1:T(8,128)(2,1)} all-gather(bf16[64,32]{0,1:T(8,128)(2,1)S(1)} %copy-done.24), channel_id=1, replica_groups=mesh['dp'=8,'sy'=2,'sx'=2] {'dp'}, dimensions={1}, use_global_device_ids=true | all-gather | bytes 36864 | tf_op jit(solution)/shard_map/all_gather | solution.py:57
  631.2 4.2 collective-permute-done.5
  635.6 1.3 collective-permute-start.6
  636.9 1.3 collective-permute-start.7
  638.2 30.6 %all_gather.36 = bf16[256,64]{0,1:T(8,128)(2,1)S(1)} all-gather(bf16[256,8]{0,1:T(8,128)(2,1)S(1)} %get-tuple-element.99), channel_id=1, replica_groups=mesh['dp'=8,'sy'=2,'sx'=2] {'dp'}, dimensions={1}, use_global_device_ids=true | all-gather | bytes 36864 | tf_op jit(solution)/shard_map/all_gather | solution.py:57
  672.7 1.7 copy.33
  679.1 36.9 %psum.169 = f32[64]{0:T(128)S(1)} all-reduce(f32[64]{0:T(128)S(1)} %get-tuple-element.150), channel_id=1, replica_groups=mesh['dp'=8,'sy'=2,'sx'=2] {'dp','sy','sx'}, use_global_device_ids=true, to_apply=%region_32.33 | all-reduce | flops 64 | bytes 512 | tf_op jit(solution)/shard_map/psum | solution.py:62
  716.2 41.0 %psum.170 = f32[64]{0:T(128)S(1)} all-reduce(f32[64]{0:T(128)S(1)} %multiply_reduce_fusion.5), channel_id=1, replica_groups=mesh['dp'=8,'sy'=2,'sx'=2] {'dp','sy','sx'}, use_global_device_ids=true, to_apply=%region_34.35 | all-reduce | flops 64 | bytes 512 | tf_op jit(solution)/shard_map/psum | solution.py:64
  758.3 39.7 %psum.171 = f32[256]{0:T(256)S(1)} all-reduce(f32[256]{0:T(256)S(1)} %get-tuple-element.152), channel_id=1, replica_groups=mesh['dp'=8,'sy'=2,'sx'=2] {'dp','sy','sx'}, use_global_device_ids=true, to_apply=%region_39.40 | all-reduce | flops 256 | bytes 2048 | tf_op jit(solution)/shard_map/psum | solution.py:62
  798.1 40.3 %psum.172 = f32[256]{0:T(256)S(1)} all-reduce(f32[256]{0:T(256)S(1)} %multiply_reduce_fusion.1), channel_id=1, replica_groups=mesh['dp'=8,'sy'=2,'sx'=2] {'dp','sy','sx'}, use_global_device_ids=true, to_apply=%region_41.42 | all-reduce | flops 256 | bytes 2048 | tf_op jit(solution)/shard_map/psum | solution.py:64
  839.7 39.7 %psum.173 = f32[64]{0:T(128)S(1)} all-reduce(f32[64]{0:T(128)S(1)} %get-tuple-element.154), channel_id=1, replica_groups=mesh['dp'=8,'sy'=2,'sx'=2] {'dp','sy','sx'}, use_global_device_ids=true, to_apply=%region_46.47 | all-reduce | flops 64 | bytes 512 | tf_op jit(solution)/shard_map/psum | solution.py:62
  879.5 40.3 %psum.174 = f32[64]{0:T(128)S(1)} all-reduce(f32[64]{0:T(128)S(1)} %multiply_reduce_fusion.4), channel_id=1, replica_groups=mesh['dp'=8,'sy'=2,'sx'=2] {'dp','sy','sx'}, use_global_device_ids=true, to_apply=%region_48.49 | all-reduce | flops 64 | bytes 512 | tf_op jit(solution)/shard_map/psum | solution.py:64
  920.9 4.2 collective-permute-start.8
  925.1 32.5 %all_gather.37 = bf16[576,64]{0,1:T(8,128)(2,1)} all-gather(bf16[576,8]{0,1:T(8,128)(2,1)S(1)} %add_convert_fusion), channel_id=1, replica_groups=mesh['dp'=8,'sy'=2,'sx'=2] {'dp'}, dimensions={1}, use_global_device_ids=true | all-gather | bytes 82944 | tf_op jit(solution)/shard_map/all_gather | solution.py:57
  959.0 4.2 collective-permute-done.9
  964.7 1.3 collective-permute-start.11
  966.0 32.8 %all_gather.38 = bf16[64,256]{0,1:T(8,128)(2,1)} all-gather(bf16[64,32]{0,1:T(8,128)(2,1)S(1)} %copy-done.23), channel_id=1, replica_groups=mesh['dp'=8,'sy'=2,'sx'=2] {'dp'}, dimensions={1}, use_global_device_ids=true | all-gather | bytes 36864 | tf_op jit(solution)/shard_map/all_gather | solution.py:57
  1008.1 36.9 %psum.175 = f32[64]{0:T(128)S(1)} all-reduce(f32[64]{0:T(128)S(1)} %get-tuple-element.156), channel_id=1, replica_groups=mesh['dp'=8,'sy'=2,'sx'=2] {'dp','sy','sx'}, use_global_device_ids=true, to_apply=%region_53.54 | all-reduce | flops 64 | bytes 512 | tf_op jit(solution)/shard_map/psum | solution.py:62
  1045.2 41.8 %psum.176 = f32[64]{0:T(128)S(1)} all-reduce(f32[64]{0:T(128)S(1)} %multiply_reduce_fusion.3), channel_id=1, replica_groups=mesh['dp'=8,'sy'=2,'sx'=2] {'dp','sy','sx'}, use_global_device_ids=true, to_apply=%region_55.56 | all-reduce | flops 64 | bytes 512 | tf_op jit(solution)/shard_map/psum | solution.py:64
  1088.1 38.9 %psum.177 = f32[256]{0:T(256)S(1)} all-reduce(f32[256]{0:T(256)S(1)} %get-tuple-element.158), channel_id=1, replica_groups=mesh['dp'=8,'sy'=2,'sx'=2] {'dp','sy','sx'}, use_global_device_ids=true, to_apply=%region_60.61 | all-reduce | flops 256 | bytes 2048 | tf_op jit(solution)/shard_map/psum | solution.py:62
  1127.2 41.2 %psum.178 = f32[256]{0:T(256)S(1)} all-reduce(f32[256]{0:T(256)S(1)} %multiply_reduce_fusion), channel_id=1, replica_groups=mesh['dp'=8,'sy'=2,'sx'=2] {'dp','sy','sx'}, use_global_device_ids=true, to_apply=%region_62.63 | all-reduce | flops 256 | bytes 2048 | tf_op jit(solution)/shard_map/psum | solution.py:64
  1169.3 6.0 psum.179
  1177.4 22.0 %psum.183 = f32[]{:T(128)} all-reduce(f32[]{:T(128)} %sub.104), channel_id=1, replica_groups=mesh['dp'=8,'sy'=2,'sx'=2] {'dp'}, use_global_device_ids=true, to_apply=%region_73.74 | all-reduce | flops 1 | bytes 8 | tf_op jit(solution)/shard_map/psum | solution.py:152
  (310 shorter events, 56.5 us)
Async XLA Ops:
  2.8 1.0 copy-start.17
  3.9 0.7 copy-start.22
  6.1 2.6 copy-start.20
  82.2 40.9 %copy-start.42 = (f32[3,2,64]{2,1,0:T(2,128)S(1)}, f32[3,2,64]{2,1,0:T(2,128)}, u32[]{:S(2)}) copy-start(f32[3,2,64]{2,1,0:T(2,128)} %param.26) | copy-start | bytes 4612
  82.4 40.7 %copy-start.41 = (f32[3,2,64]{2,1,0:T(2,128)S(1)}, f32[3,2,64]{2,1,0:T(2,128)}, u32[]{:S(2)}) copy-start(f32[3,2,64]{2,1,0:T(2,128)} %param.27) | copy-start | bytes 4612
  124.6 5.6 copy-start.9
  124.7 180.1 %collective-permute-start = (bf16[1,1,28,64]{3,2,1,0:T(8,128)(2,1)S(1)}, bf16[1,1,28,64]{3,2,1,0:T(8,128)(2,1)S(1)}, u32[]{:S(2)}, u32[]{:S(2)}) collective-permute-start(bf16[1,1,28,64]{3,2,1,0:T(8,128)(2,1)S(1)} %get-tuple-element.86), channel_id=1, source_target_pairs={{0,2},{1,3},{4,6},{5,7},{8,10},{9,11},{12,14},{13,15},{16,18},{17,... | collective-permute-start | bytes 10760 | tf_op jit(solution)/shard_map/ppermute | solution.py:20
  128.8 175.9 %collective-permute-start.1 = (bf16[1,1,28,64]{3,2,1,0:T(8,128)(2,1)S(1)}, bf16[1,1,28,64]{3,2,1,0:T(8,128)(2,1)S(1)}, u32[]{:S(2)}, u32[]{:S(2)}) collective-permute-start(bf16[1,1,28,64]{3,2,1,0:T(8,128)(2,1)S(1)} %get-tuple-element.85), channel_id=1, source_target_pairs={{2,0},{3,1},{6,4},{7,5},{10,8},{11,9},{14,12},{15,13},{18,16},{19,... | collective-permute-start | bytes 10760 | tf_op jit(solution)/shard_map/ppermute | solution.py:22
  130.6 32.7 %copy-start.18 = (bf16[2,3,64,32]{2,3,1,0:T(8,128)(2,1)S(1)}, bf16[2,3,64,32]{2,3,1,0:T(8,128)(2,1)}, u32[]{:S(2)}) copy-start(bf16[2,3,64,32]{2,3,1,0:T(8,128)(2,1)} %param.24) | copy-start | bytes 73732
  163.3 0.7 copy-start.21
  164.0 0.7 copy-start.43
  164.7 0.7 copy-start.44
  199.1 0.9 copy-start
  199.2 0.9 copy-start.16
  304.9 36.4 %collective-permute-start.2 = (bf16[1,30,1,64]{3,2,1,0:T(2,128)(2,1)S(1)}, bf16[1,30,1,64]{3,2,1,0:T(2,128)(2,1)S(1)}, u32[]{:S(2)}, u32[]{:S(2)}) collective-permute-start(bf16[1,30,1,64]{3,2,1,0:T(2,128)(2,1)S(1)} %get-tuple-element.71), channel_id=1, source_target_pairs={{0,1},{2,3},{4,5},{6,7},{8,9},{10,11},{12,13},{14,15},{16,17},{18,... | collective-permute-start | bytes 11528 | tf_op jit(solution)/shard_map/ppermute | solution.py:20
  306.2 35.1 %collective-permute-start.3 = (bf16[1,30,1,64]{3,2,1,0:T(2,128)(2,1)S(1)}, bf16[1,30,1,64]{3,2,1,0:T(2,128)(2,1)S(1)}, u32[]{:S(2)}, u32[]{:S(2)}) collective-permute-start(bf16[1,30,1,64]{3,2,1,0:T(2,128)(2,1)S(1)} %get-tuple-element.70), channel_id=1, source_target_pairs={{1,0},{3,2},{5,4},{7,6},{9,8},{11,10},{13,12},{15,14},{17,16},{19,... | collective-permute-start | bytes 11528 | tf_op jit(solution)/shard_map/ppermute | solution.py:22
  342.8 0.9 copy-start.3
  343.7 0.9 copy-start.6
  346.1 0.9 copy-start.1
  347.0 0.9 copy-start.11
  385.8 43.0 %copy-start.14 = (bf16[64,256]{0,1:T(8,128)(2,1)S(1)}, bf16[64,256]{0,1:T(8,128)(2,1)}, u32[]{:S(2)}) copy-start(bf16[64,256]{0,1:T(8,128)(2,1)} %all_gather.32) | copy-start | bytes 98308
  428.8 0.7 copy-start.50
  468.0 42.0 %copy-start.38 = (f32[1,256]{1,0:T(1,128)S(1)}, f32[1,256]{1,0:T(1,128)}, u32[]{:S(2)}) copy-start(f32[1,256]{1,0:T(1,128)} %get-tuple-element.108) | copy-start | bytes 3076
  510.0 0.7 copy-start.37
  510.7 0.8 copy-start.19
  593.0 4.3 copy-start.24
  593.1 38.0 %collective-permute-start.4 = (bf16[1,1,28,64]{3,2,1,0:T(8,128)(2,1)S(1)}, bf16[1,1,28,64]{3,2,1,0:T(8,128)(2,1)S(1)}, u32[]{:S(2)}, u32[]{:S(2)}) collective-permute-start(bf16[1,1,28,64]{3,2,1,0:T(8,128)(2,1)S(1)} %get-tuple-element.81), channel_id=1, source_target_pairs={{0,2},{1,3},{4,6},{5,7},{8,10},{9,11},{12,14},{13,15},{16,18},{17,... | collective-permute-start | bytes 10760 | tf_op jit(solution)/shard_map/ppermute | solution.py:20
  629.9 5.5 collective-permute-start.5
  635.6 34.3 %collective-permute-start.6 = (bf16[1,30,1,64]{3,2,1,0:T(2,128)(2,1)S(1)}, bf16[1,30,1,64]{3,2,1,0:T(2,128)(2,1)S(1)}, u32[]{:S(2)}, u32[]{:S(2)}) collective-permute-start(bf16[1,30,1,64]{3,2,1,0:T(2,128)(2,1)S(1)} %get-tuple-element.66), channel_id=1, source_target_pairs={{0,1},{2,3},{4,5},{6,7},{8,9},{10,11},{12,13},{14,15},{16,17},{18,... | collective-permute-start | bytes 11528 | tf_op jit(solution)/shard_map/ppermute | solution.py:20
  636.9 33.0 %collective-permute-start.7 = (bf16[1,30,1,64]{3,2,1,0:T(2,128)(2,1)S(1)}, bf16[1,30,1,64]{3,2,1,0:T(2,128)(2,1)S(1)}, u32[]{:S(2)}, u32[]{:S(2)}) collective-permute-start(bf16[1,30,1,64]{3,2,1,0:T(2,128)(2,1)S(1)} %get-tuple-element.65), channel_id=1, source_target_pairs={{1,0},{3,2},{5,4},{7,6},{9,8},{11,10},{13,12},{15,14},{17,16},{19,... | collective-permute-start | bytes 11528 | tf_op jit(solution)/shard_map/ppermute | solution.py:22
  674.5 0.9 copy-start.4
  675.4 0.9 copy-start.7
  677.8 0.9 copy-start.10
  716.0 41.2 %copy-start.13 = (bf16[64,256]{0,1:T(8,128)(2,1)S(1)}, bf16[64,256]{0,1:T(8,128)(2,1)}, u32[]{:S(2)}) copy-start(bf16[64,256]{0,1:T(8,128)(2,1)} %all_gather.35) | copy-start | bytes 98308
  798.0 40.4 %copy-start.36 = (f32[1,256]{1,0:T(1,128)S(1)}, f32[1,256]{1,0:T(1,128)}, u32[]{:S(2)}) copy-start(f32[1,256]{1,0:T(1,128)} %get-tuple-element.107) | copy-start | bytes 3076
  838.4 0.7 copy-start.35
  920.9 38.0 %collective-permute-start.8 = (bf16[1,1,28,64]{3,2,1,0:T(8,128)(2,1)S(1)}, bf16[1,1,28,64]{3,2,1,0:T(8,128)(2,1)S(1)}, u32[]{:S(2)}, u32[]{:S(2)}) collective-permute-start(bf16[1,1,28,64]{3,2,1,0:T(8,128)(2,1)S(1)} %get-tuple-element.76), channel_id=1, source_target_pairs={{0,2},{1,3},{4,6},{5,7},{8,10},{9,11},{12,14},{13,15},{16,18},{17,... | collective-permute-start | bytes 10760 | tf_op jit(solution)/shard_map/ppermute | solution.py:20
  957.6 5.5 collective-permute-start.9
  963.3 2.6 copy-start.23
  963.4 37.7 %collective-permute-start.10 = (bf16[1,30,1,64]{3,2,1,0:T(2,128)(2,1)S(1)}, bf16[1,30,1,64]{3,2,1,0:T(2,128)(2,1)S(1)}, u32[]{:S(2)}, u32[]{:S(2)}) collective-permute-start(bf16[1,30,1,64]{3,2,1,0:T(2,128)(2,1)S(1)} %get-tuple-element.61), channel_id=1, source_target_pairs={{0,1},{2,3},{4,5},{6,7},{8,9},{10,11},{12,13},{14,15},{16,17},{18,... | collective-permute-start | bytes 11528 | tf_op jit(solution)/shard_map/ppermute | solution.py:20
  964.7 36.4 %collective-permute-start.11 = (bf16[1,30,1,64]{3,2,1,0:T(2,128)(2,1)S(1)}, bf16[1,30,1,64]{3,2,1,0:T(2,128)(2,1)S(1)}, u32[]{:S(2)}, u32[]{:S(2)}) collective-permute-start(bf16[1,30,1,64]{3,2,1,0:T(2,128)(2,1)S(1)} %get-tuple-element.60), channel_id=1, source_target_pairs={{1,0},{3,2},{5,4},{7,6},{9,8},{11,10},{13,12},{15,14},{17,16},{19,... | collective-permute-start | bytes 11528 | tf_op jit(solution)/shard_map/ppermute | solution.py:22
  1002.6 0.9 copy-start.5
  1003.5 0.9 copy-start.8
  1005.9 0.9 copy-start.2
  1006.8 0.9 copy-start.12
  1045.0 42.0 %copy-start.15 = (bf16[64,256]{0,1:T(8,128)(2,1)S(1)}, bf16[64,256]{0,1:T(8,128)(2,1)}, u32[]{:S(2)}) copy-start(bf16[64,256]{0,1:T(8,128)(2,1)} %all_gather.38) | copy-start | bytes 98308
  1127.0 41.3 %copy-start.40 = (f32[1,256]{1,0:T(1,128)S(1)}, f32[1,256]{1,0:T(1,128)}, u32[]{:S(2)}) copy-start(f32[1,256]{1,0:T(1,128)} %get-tuple-element.109) | copy-start | bytes 3076
  1168.3 0.7 copy-start.39
  (21 other events, 13.0 us)
where the time goes:
time: 1210 us; the launch traced here: 1200 us
  blocking collectives  1100 us (91%)
  local copies, waits for them, and re-layouts  39.7 us (3%)
  starting transfers between devices  24.1 us (2%)
  other arithmetic  17.3 us (1%)
    psum x9, blocking collectives, normalize(): lax.psum(jnp.sum(centred * centred, axis=0), ('dp', 'sy', 'sx')) / count  372 us
    psum x9, blocking collectives, normalize(): mean = lax.psum(jnp.sum(y, axis=0), ('dp', 'sy', 'sx')) / count  345 us
    all_gather x9, blocking collectives, perturbed_product(): lax.all_gather(local, 'dp', axis=1, tiled=True)  291 us
    psum x1, blocking collectives, per_device(): lax.psum((jnp.sum(jnp.square(w_class.astype(jnp.float32)), axis=0), jnp.s...  36.1 us
    all_gather x1, blocking collectives, per_device(): lax.all_gather(local_class, 'dp', axis=0, tiled=True)  31.2 us
  transfers between devices with their start and end apart: 12, of which 2 were waited for; matrix products, arithmetic and copies ran while one was open for 1% of the time, Pallas kernels for 0%

commit v1 on v0

--- a/solution.py
+++ b/solution.py
@@ -61,7 +61,7 @@
 def normalize(y, gain, shift, count):
     mean = lax.psum(jnp.sum(y, axis=0), ("dp", "sy", "sx")) / count
     centred = y - mean
-    var = lax.psum(jnp.sum(centred * centred, axis=0), ("dp", "sy", "sx")) / count
+    var = lax.psum(lax.psum(jnp.sum(centred * centred, axis=0), ("sy", "sx")), "dp") / count
     return centred * lax.rsqrt(var + EPS_BN) * gain + shift
 
 

time: 1210 us -> 999 us (0.83)
  blocking collectives: 1100 us -> 924 us
  local copies, waits for them, and re-layouts: 39.7 us -> 11 us
    psum x10 -> x18, blocking collectives: 408 us -> 257 us  [the longest x9 204 us: normalize(): lax.psum(lax.psum(jnp.sum(centred * centred, axis=0), ('sy', 'sx')), 'dp')]
    unnamed x138 -> x48, local copies, waits for them, and re-layouts: 21.2 us -> 1.55 us
    all_gather x9, blocking collectives: 291 us -> 277 us  [perturbed_product(): lax.all_gather(local, 'dp', axis=1, tiled=True)]
where the time goes in v1:
time: 999 us; the launch traced here: 996 us
  blocking collectives  924 us (92%)
  starting transfers between devices  25.2 us (3%)
  other arithmetic  17.5 us (2%)
  local copies, waits for them, and re-layouts  11 us (1%)
    psum x9, blocking collectives, normalize(): mean = lax.psum(jnp.sum(y, axis=0), ('dp', 'sy', 'sx')) / count  334 us
    all_gather x9, blocking collectives, perturbed_product(): lax.all_gather(local, 'dp', axis=1, tiled=True)  277 us
    psum x9, blocking collectives, normalize(): lax.psum(lax.psum(jnp.sum(centred * centred, axis=0), ('sy', 'sx')), 'dp')  204 us
    psum x9, blocking collectives, normalize(): lax.psum(jnp.sum(centred * centred, axis=0), ('sy', 'sx'))  52.5 us
    all_gather x1, blocking collectives, per_device(): lax.all_gather(local_class, 'dp', axis=0, tiled=True)  31.4 us
  transfers between devices with their start and end apart: 12, of which 2 were waited for; matrix products, arithmetic and copies ran while one was open for 1% of the time, Pallas kernels for 0%

profile of v1, /device:TPU:0, one launch (start us, length us, event | category | flops | bytes accessed | tf_op | source)
XLA Modules:
  0.0 996.5 jit_solution(6861950664299770670)
XLA Ops:
  8.9 32.4 %all_gather.30 = bf16[256,64]{0,1:T(8,128)(2,1)S(1)} all-gather(bf16[256,8]{0,1:T(8,128)(2,1)S(1)} %get-tuple-element.101), channel_id=1, replica_groups=mesh['dp'=8,'sy'=2,'sx'=2] {'dp'}, dimensions={1}, use_global_device_ids=true | all-gather | bytes 36864 | tf_op jit(solution)/shard_map/all_gather | solution.py:57
  42.8 39.6 %psum.224 = f32[64]{0:T(128)S(1)} all-reduce(f32[64]{0:T(128)S(1)} %get-tuple-element.143), channel_id=1, replica_groups=mesh['dp'=8,'sy'=2,'sx'=2] {'dp','sy','sx'}, use_global_device_ids=true, to_apply=%region_4.0 | all-reduce | flops 64 | bytes 512 | tf_op jit(solution)/shard_map/psum | solution.py:62
  82.6 5.8 psum.225
  88.4 20.4 %psum.226 = f32[64]{0:T(128)S(1)} all-reduce(f32[64]{0:T(128)S(1)} %psum.225), channel_id=1, replica_groups=mesh['dp'=8,'sy'=2,'sx'=2] {'dp'}, use_global_device_ids=true, to_apply=%region_7.0 | all-reduce | flops 64 | bytes 512 | tf_op jit(solution)/shard_map/psum | solution.py:64
  109.3 1.4 collective-permute-start.1
  110.7 4.5 collective-permute-start
  118.1 30.5 %all_gather.31 = bf16[576,64]{0,1:T(8,128)(2,1)S(1)} all-gather(bf16[576,8]{0,1:T(8,128)(2,1)S(1)} %add_convert_fusion.2), channel_id=1, replica_groups=mesh['dp'=8,'sy'=2,'sx'=2] {'dp'}, dimensions={1}, use_global_device_ids=true | all-gather | bytes 82944 | tf_op jit(solution)/shard_map/all_gather | solution.py:57
  148.7 30.5 %all_gather.34 = bf16[576,64]{0,1:T(8,128)(2,1)S(1)} all-gather(bf16[576,8]{0,1:T(8,128)(2,1)S(1)} %add_convert_fusion.1), channel_id=1, replica_groups=mesh['dp'=8,'sy'=2,'sx'=2] {'dp'}, dimensions={1}, use_global_device_ids=true | all-gather | bytes 82944 | tf_op jit(solution)/shard_map/all_gather | solution.py:57
  182.0 30.6 %all_gather.33 = bf16[256,64]{0,1:T(8,128)(2,1)S(1)} all-gather(bf16[256,8]{0,1:T(8,128)(2,1)S(1)} %get-tuple-element.102), channel_id=1, replica_groups=mesh['dp'=8,'sy'=2,'sx'=2] {'dp'}, dimensions={1}, use_global_device_ids=true | all-gather | bytes 36864 | tf_op jit(solution)/shard_map/all_gather | solution.py:57
  214.1 3.0 collective-permute-start.2
  217.1 30.5 %all_gather.32 = bf16[64,256]{0,1:T(8,128)(2,1)S(1)} all-gather(bf16[64,32]{0,1:T(8,128)(2,1)S(1)} %get-tuple-element.96), channel_id=1, replica_groups=mesh['dp'=8,'sy'=2,'sx'=2] {'dp'}, dimensions={1}, use_global_device_ids=true | all-gather | bytes 36864 | tf_op jit(solution)/shard_map/all_gather | solution.py:57
  250.6 36.8 %psum.227 = f32[64]{0:T(128)S(1)} all-reduce(f32[64]{0:T(128)S(1)} %get-tuple-element.145), channel_id=1, replica_groups=mesh['dp'=8,'sy'=2,'sx'=2] {'dp','sy','sx'}, use_global_device_ids=true, to_apply=%region_12.13 | all-reduce | flops 64 | bytes 512 | tf_op jit(solution)/shard_map/psum | solution.py:62
  287.6 5.8 psum.228
  293.4 21.0 %psum.229 = f32[64]{0:T(128)S(1)} all-reduce(f32[64]{0:T(128)S(1)} %psum.228), channel_id=1, replica_groups=mesh['dp'=8,'sy'=2,'sx'=2] {'dp'}, use_global_device_ids=true, to_apply=%region_15.16 | all-reduce | flops 64 | bytes 512 | tf_op jit(solution)/shard_map/psum | solution.py:64
  314.9 36.8 %psum.230 = f32[256]{0:T(256)S(1)} all-reduce(f32[256]{0:T(256)S(1)} %get-tuple-element.147), channel_id=1, replica_groups=mesh['dp'=8,'sy'=2,'sx'=2] {'dp','sy','sx'}, use_global_device_ids=true, to_apply=%region_20.21 | all-reduce | flops 256 | bytes 2048 | tf_op jit(solution)/shard_map/psum | solution.py:62
  351.9 5.8 psum.231
  357.8 21.0 %psum.232 = f32[256]{0:T(256)S(1)} all-reduce(f32[256]{0:T(256)S(1)} %psum.231), channel_id=1, replica_groups=mesh['dp'=8,'sy'=2,'sx'=2] {'dp'}, use_global_device_ids=true, to_apply=%region_23.24 | all-reduce | flops 256 | bytes 2048 | tf_op jit(solution)/shard_map/psum | solution.py:64
  379.4 36.8 %psum.233 = f32[64]{0:T(128)S(1)} all-reduce(f32[64]{0:T(128)S(1)} %get-tuple-element.149), channel_id=1, replica_groups=mesh['dp'=8,'sy'=2,'sx'=2] {'dp','sy','sx'}, use_global_device_ids=true, to_apply=%region_28.29 | all-reduce | flops 64 | bytes 512 | tf_op jit(solution)/shard_map/psum | solution.py:62
  416.4 5.8 psum.234
  422.3 21.0 %psum.235 = f32[64]{0:T(128)S(1)} all-reduce(f32[64]{0:T(128)S(1)} %psum.234), channel_id=1, replica_groups=mesh['dp'=8,'sy'=2,'sx'=2] {'dp'}, use_global_device_ids=true, to_apply=%region_31.32 | all-reduce | flops 64 | bytes 512 | tf_op jit(solution)/shard_map/psum | solution.py:64
  443.7 1.8 collective-permute-start.4
  445.6 30.6 %all_gather.36 = bf16[256,64]{0,1:T(8,128)(2,1)S(1)} all-gather(bf16[256,8]{0,1:T(8,128)(2,1)S(1)} %get-tuple-element.100), channel_id=1, replica_groups=mesh['dp'=8,'sy'=2,'sx'=2] {'dp'}, dimensions={1}, use_global_device_ids=true | all-gather | bytes 36864 | tf_op jit(solution)/shard_map/all_gather | solution.py:57
  477.5 4.2 collective-permute-done.5
  483.2 3.0 collective-permute-start.6
  486.2 30.7 %all_gather.35 = bf16[64,256]{0,1:T(8,128)(2,1)S(1)} all-gather(bf16[64,32]{0,1:T(8,128)(2,1)S(1)} %get-tuple-element.94), channel_id=1, replica_groups=mesh['dp'=8,'sy'=2,'sx'=2] {'dp'}, dimensions={1}, use_global_device_ids=true | all-gather | bytes 36864 | tf_op jit(solution)/shard_map/all_gather | solution.py:57
  519.8 36.8 %psum.236 = f32[64]{0:T(128)S(1)} all-reduce(f32[64]{0:T(128)S(1)} %get-tuple-element.151), channel_id=1, replica_groups=mesh['dp'=8,'sy'=2,'sx'=2] {'dp','sy','sx'}, use_global_device_ids=true, to_apply=%region_36.37 | all-reduce | flops 64 | bytes 512 | tf_op jit(solution)/shard_map/psum | solution.py:62
  556.8 5.8 psum.237
  562.7 21.0 %psum.238 = f32[64]{0:T(128)S(1)} all-reduce(f32[64]{0:T(128)S(1)} %psum.237), channel_id=1, replica_groups=mesh['dp'=8,'sy'=2,'sx'=2] {'dp'}, use_global_device_ids=true, to_apply=%region_39.40 | all-reduce | flops 64 | bytes 512 | tf_op jit(solution)/shard_map/psum | solution.py:64
  584.2 36.8 %psum.239 = f32[256]{0:T(256)S(1)} all-reduce(f32[256]{0:T(256)S(1)} %get-tuple-element.153), channel_id=1, replica_groups=mesh['dp'=8,'sy'=2,'sx'=2] {'dp','sy','sx'}, use_global_device_ids=true, to_apply=%region_44.45 | all-reduce | flops 256 | bytes 2048 | tf_op jit(solution)/shard_map/psum | solution.py:62
  621.2 5.8 psum.240
  627.0 21.0 %psum.241 = f32[256]{0:T(256)S(1)} all-reduce(f32[256]{0:T(256)S(1)} %psum.240), channel_id=1, replica_groups=mesh['dp'=8,'sy'=2,'sx'=2] {'dp'}, use_global_device_ids=true, to_apply=%region_47.48 | all-reduce | flops 256 | bytes 2048 | tf_op jit(solution)/shard_map/psum | solution.py:64
  648.6 36.8 %psum.242 = f32[64]{0:T(128)S(1)} all-reduce(f32[64]{0:T(128)S(1)} %get-tuple-element.155), channel_id=1, replica_groups=mesh['dp'=8,'sy'=2,'sx'=2] {'dp','sy','sx'}, use_global_device_ids=true, to_apply=%region_52.53 | all-reduce | flops 64 | bytes 512 | tf_op jit(solution)/shard_map/psum | solution.py:62
  685.7 5.8 psum.243
  691.5 21.0 %psum.244 = f32[64]{0:T(128)S(1)} all-reduce(f32[64]{0:T(128)S(1)} %psum.243), channel_id=1, replica_groups=mesh['dp'=8,'sy'=2,'sx'=2] {'dp'}, use_global_device_ids=true, to_apply=%region_55.56 | all-reduce | flops 64 | bytes 512 | tf_op jit(solution)/shard_map/psum | solution.py:64
  713.0 1.8 collective-permute-start.8
  714.8 30.5 %all_gather.37 = bf16[576,64]{0,1:T(8,128)(2,1)S(1)} all-gather(bf16[576,8]{0,1:T(8,128)(2,1)S(1)} %add_convert_fusion), channel_id=1, replica_groups=mesh['dp'=8,'sy'=2,'sx'=2] {'dp'}, dimensions={1}, use_global_device_ids=true | all-gather | bytes 82944 | tf_op jit(solution)/shard_map/all_gather | solution.py:57
  746.7 4.2 collective-permute-done.9
  752.4 3.0 collective-permute-start.10
  755.4 30.5 %all_gather.38 = bf16[64,256]{0,1:T(8,128)(2,1)S(1)} all-gather(bf16[64,32]{0,1:T(8,128)(2,1)S(1)} %get-tuple-element.95), channel_id=1, replica_groups=mesh['dp'=8,'sy'=2,'sx'=2] {'dp'}, dimensions={1}, use_global_device_ids=true | all-gather | bytes 36864 | tf_op jit(solution)/shard_map/all_gather | solution.py:57
  789.5 36.8 %psum.245 = f32[64]{0:T(128)S(1)} all-reduce(f32[64]{0:T(128)S(1)} %get-tuple-element.157), channel_id=1, replica_groups=mesh['dp'=8,'sy'=2,'sx'=2] {'dp','sy','sx'}, use_global_device_ids=true, to_apply=%region_60.61 | all-reduce | flops 64 | bytes 512 | tf_op jit(solution)/shard_map/psum | solution.py:62
  826.5 5.8 psum.246
  832.3 21.0 %psum.247 = f32[64]{0:T(128)S(1)} all-reduce(f32[64]{0:T(128)S(1)} %psum.246), channel_id=1, replica_groups=mesh['dp'=8,'sy'=2,'sx'=2] {'dp'}, use_global_device_ids=true, to_apply=%region_63.64 | all-reduce | flops 64 | bytes 512 | tf_op jit(solution)/shard_map/psum | solution.py:64
  853.8 36.8 %psum.248 = f32[256]{0:T(256)S(1)} all-reduce(f32[256]{0:T(256)S(1)} %get-tuple-element.159), channel_id=1, replica_groups=mesh['dp'=8,'sy'=2,'sx'=2] {'dp','sy','sx'}, use_global_device_ids=true, to_apply=%region_68.69 | all-reduce | flops 256 | bytes 2048 | tf_op jit(solution)/shard_map/psum | solution.py:62
  890.8 5.8 psum.249
  896.7 36.7 %all-reduce = (f32[256]{0:T(256)S(1)}, f32[1000]{0:T(1024)S(1)}, f32[1000]{0:T(1024)S(1)}, f32[1000]{0:T(1024)S(1)}) all-reduce(f32[256]{0:T(256)S(1)} %psum.249, f32[1000]{0:T(1024)S(1)} %get-tuple-element.4, f32[1000]{0:T(1024)S(1)} %fusion.12, f32[1000]{0:T(1024)S(1)} %get-tuple-element.3), channel_id=1, replica_groups=mesh['dp'=8,'sy'=2,'sx'=2] {'dp'}, use_global_device_ids=true, to_apply=%region_71.72 | all-reduce | flops 3256 | bytes 26048 | tf_op jit(solution)/shard_map/psum | solution.py:64
  933.7 5.8 psum.251
  940.8 31.4 %all_gather.39 = bf16[256,1000]{1,0:T(8,128)(2,1)S(1)} all-gather(bf16[32,1000]{1,0:T(8,128)(2,1)S(1)} %fusion.14), channel_id=1, replica_groups=mesh['dp'=8,'sy'=2,'sx'=2] {'dp'}, dimensions={0}, use_global_device_ids=true | all-gather | bytes 576000 | tf_op jit(solution)/shard_map/all_gather | solution.py:145
  974.3 18.4 %psum.255 = f32[]{:T(128)} all-reduce(f32[]{:T(128)} %sub.104), channel_id=1, replica_groups=mesh['dp'=8,'sy'=2,'sx'=2] {'dp'}, use_global_device_ids=true, to_apply=%region_82.83 | all-reduce | flops 1 | bytes 8 | tf_op jit(solution)/shard_map/psum | solution.py:152
  (229 shorter events, 38.9 us)
Async XLA Ops:
  2.7 0.9 copy-start.5
  7.5 1.3 copy-start.7
  82.4 26.5 %copy-start.9 = (f32[3,2,64]{2,1,0:T(2,128)S(1)}, f32[3,2,64]{2,1,0:T(2,128)}, u32[]{:S(2)}) copy-start(f32[3,2,64]{2,1,0:T(2,128)} %param.26) | copy-start | bytes 4612
  82.6 26.3 %copy-start.8 = (f32[3,2,64]{2,1,0:T(2,128)S(1)}, f32[3,2,64]{2,1,0:T(2,128)}, u32[]{:S(2)}) copy-start(f32[3,2,64]{2,1,0:T(2,128)} %param.27) | copy-start | bytes 4612
  109.2 6.1 copy-start.3
  109.3 6.0 copy-start.1
  109.3 103.3 %collective-permute-start.1 = (bf16[1,1,28,64]{3,2,1,0:T(8,128)(2,1)S(1)}, bf16[1,1,28,64]{3,2,1,0:T(8,128)(2,1)S(1)}, u32[]{:S(2)}, u32[]{:S(2)}) collective-permute-start(bf16[1,1,28,64]{3,2,1,0:T(8,128)(2,1)S(1)} %get-tuple-element.86), channel_id=1, source_target_pairs={{2,0},{3,1},{6,4},{7,5},{10,8},{11,9},{14,12},{15,13},{18,16},{19,... | collective-permute-start | bytes 10760 | tf_op jit(solution)/shard_map/ppermute | solution.py:22
  110.7 101.9 %collective-permute-start = (bf16[1,1,28,64]{3,2,1,0:T(8,128)(2,1)S(1)}, bf16[1,1,28,64]{3,2,1,0:T(8,128)(2,1)S(1)}, u32[]{:S(2)}, u32[]{:S(2)}) collective-permute-start(bf16[1,1,28,64]{3,2,1,0:T(8,128)(2,1)S(1)} %get-tuple-element.87), channel_id=1, source_target_pairs={{0,2},{1,3},{4,6},{5,7},{8,10},{9,11},{12,14},{13,15},{16,18},{17,... | collective-permute-start | bytes 10760 | tf_op jit(solution)/shard_map/ppermute | solution.py:20
  115.3 0.7 copy-start.6
  115.3 0.9 copy-start.4
  115.3 1.1 copy-start.10
  115.3 1.1 copy-start.11
  115.4 1.1 copy-start.2
  116.1 0.9 copy-start
  212.8 35.3 %collective-permute-start.3 = (bf16[1,30,1,64]{3,2,1,0:T(2,128)(2,1)S(1)}, bf16[1,30,1,64]{3,2,1,0:T(2,128)(2,1)S(1)}, u32[]{:S(2)}, u32[]{:S(2)}) collective-permute-start(bf16[1,30,1,64]{3,2,1,0:T(2,128)(2,1)S(1)} %get-tuple-element.71), channel_id=1, source_target_pairs={{1,0},{3,2},{5,4},{7,6},{9,8},{11,10},{13,12},{15,14},{17,16},{19,... | collective-permute-start | bytes 11528 | tf_op jit(solution)/shard_map/ppermute | solution.py:22
  214.1 34.0 %collective-permute-start.2 = (bf16[1,30,1,64]{3,2,1,0:T(2,128)(2,1)S(1)}, bf16[1,30,1,64]{3,2,1,0:T(2,128)(2,1)S(1)}, u32[]{:S(2)}, u32[]{:S(2)}) collective-permute-start(bf16[1,30,1,64]{3,2,1,0:T(2,128)(2,1)S(1)} %get-tuple-element.72), channel_id=1, source_target_pairs={{0,1},{2,3},{4,5},{6,7},{8,9},{10,11},{12,13},{14,15},{16,17},{18,... | collective-permute-start | bytes 11528 | tf_op jit(solution)/shard_map/ppermute | solution.py:20
  443.7 33.8 %collective-permute-start.4 = (bf16[1,1,28,64]{3,2,1,0:T(8,128)(2,1)S(1)}, bf16[1,1,28,64]{3,2,1,0:T(8,128)(2,1)S(1)}, u32[]{:S(2)}, u32[]{:S(2)}) collective-permute-start(bf16[1,1,28,64]{3,2,1,0:T(8,128)(2,1)S(1)} %get-tuple-element.82), channel_id=1, source_target_pairs={{0,2},{1,3},{4,6},{5,7},{8,10},{9,11},{12,14},{13,15},{16,18},{17,... | collective-permute-start | bytes 10760 | tf_op jit(solution)/shard_map/ppermute | solution.py:20
  476.2 5.5 collective-permute-start.5
  481.9 35.5 %collective-permute-start.7 = (bf16[1,30,1,64]{3,2,1,0:T(2,128)(2,1)S(1)}, bf16[1,30,1,64]{3,2,1,0:T(2,128)(2,1)S(1)}, u32[]{:S(2)}, u32[]{:S(2)}) collective-permute-start(bf16[1,30,1,64]{3,2,1,0:T(2,128)(2,1)S(1)} %get-tuple-element.66), channel_id=1, source_target_pairs={{1,0},{3,2},{5,4},{7,6},{9,8},{11,10},{13,12},{15,14},{17,16},{19,... | collective-permute-start | bytes 11528 | tf_op jit(solution)/shard_map/ppermute | solution.py:22
  483.2 34.2 %collective-permute-start.6 = (bf16[1,30,1,64]{3,2,1,0:T(2,128)(2,1)S(1)}, bf16[1,30,1,64]{3,2,1,0:T(2,128)(2,1)S(1)}, u32[]{:S(2)}, u32[]{:S(2)}) collective-permute-start(bf16[1,30,1,64]{3,2,1,0:T(2,128)(2,1)S(1)} %get-tuple-element.67), channel_id=1, source_target_pairs={{0,1},{2,3},{4,5},{6,7},{8,9},{10,11},{12,13},{14,15},{16,17},{18,... | collective-permute-start | bytes 11528 | tf_op jit(solution)/shard_map/ppermute | solution.py:20
  713.0 33.7 %collective-permute-start.8 = (bf16[1,1,28,64]{3,2,1,0:T(8,128)(2,1)S(1)}, bf16[1,1,28,64]{3,2,1,0:T(8,128)(2,1)S(1)}, u32[]{:S(2)}, u32[]{:S(2)}) collective-permute-start(bf16[1,1,28,64]{3,2,1,0:T(8,128)(2,1)S(1)} %get-tuple-element.77), channel_id=1, source_target_pairs={{0,2},{1,3},{4,6},{5,7},{8,10},{9,11},{12,14},{13,15},{16,18},{17,... | collective-permute-start | bytes 10760 | tf_op jit(solution)/shard_map/ppermute | solution.py:20
  745.4 5.5 collective-permute-start.9
  751.0 36.0 %collective-permute-start.11 = (bf16[1,30,1,64]{3,2,1,0:T(2,128)(2,1)S(1)}, bf16[1,30,1,64]{3,2,1,0:T(2,128)(2,1)S(1)}, u32[]{:S(2)}, u32[]{:S(2)}) collective-permute-start(bf16[1,30,1,64]{3,2,1,0:T(2,128)(2,1)S(1)} %get-tuple-element.61), channel_id=1, source_target_pairs={{1,0},{3,2},{5,4},{7,6},{9,8},{11,10},{13,12},{15,14},{17,16},{19,... | collective-permute-start | bytes 11528 | tf_op jit(solution)/shard_map/ppermute | solution.py:22
  752.4 34.7 %collective-permute-start.10 = (bf16[1,30,1,64]{3,2,1,0:T(2,128)(2,1)S(1)}, bf16[1,30,1,64]{3,2,1,0:T(2,128)(2,1)S(1)}, u32[]{:S(2)}, u32[]{:S(2)}) collective-permute-start(bf16[1,30,1,64]{3,2,1,0:T(2,128)(2,1)S(1)} %get-tuple-element.62), channel_id=1, source_target_pairs={{0,1},{2,3},{4,5},{6,7},{8,9},{10,11},{12,13},{14,15},{16,17},{18,... | collective-permute-start | bytes 11528 | tf_op jit(solution)/shard_map/ppermute | solution.py:20
